TPU v7x, 256 devices: a whole 4x4x8 slice. The times are simulated.
256 devices in a mesh: ops: 64 (over x, z, core), sec: 4 (over y).
Axes of the slice: x: 4, y: 4, z: 8, core: 2. Of those that a mesh axis runs over, the one named last changes fastest.
Arguments:
- operators: bfloat16 [128, 8, 768, 768], P('ops', 'sec'), may hold values from -6 to 6
- basis: bfloat16 [8, 768, 768], P('sec'), may hold values from -0.21875 to 0.21875
- shift: int32 [128], replicated, may hold values from -1 to 1
- dest: int32 [128], replicated, may hold values from 0 to 127, each once
- sector_sizes: int32 [8], replicated, may hold values from 384 to 768
Outputs:
- renormalized: bfloat16 [128, 8, 768, 768], P('ops', 'sec')
Inputs may be any that keep to these rules, and one draw needn't show every extreme that they name: `shift`: each pair's offset is -1, 0 or 1. dest names every index of 0 to 127 once.
All inputs are finite; a program needn't handle non-finite values.
Results may differ from a plain program's by a relative error of at most 0.0049.
Values may be sent and summed in bfloat16 or wider, within the bound.
No kernel may reach another device: no remote copies, remote signals or barrier semaphores. Data moves between devices by JAX's collectives and lax.ppermute only.
A program may use at most 128 MiB of HBM per device.

v0:
```python
import functools

import jax
import jax.numpy as jnp
from jax import lax
from jax.experimental import pallas as pl
from jax.experimental.pallas import tpu as pltpu
from jax.sharding import PartitionSpec as P

HBM = pl.BlockSpec(memory_space=pl.ANY)
VMEM = pl.BlockSpec(memory_space=pltpu.VMEM)
SMEM = pl.BlockSpec(memory_space=pltpu.SMEM)
LANES = 128
SUBLANES = 8
STEP = 16
TILE = 256
CHOICES = 4


def times_transposed(left, right):
    return lax.dot_general(
        left, right, (((1,), (1,)), ((), ())), preferred_element_type=jnp.float32
    )


def regions_of(sizes_ref, sectors, lanes):
    first = lax.axis_index("sec") * sectors
    heights = [
        pl.cdiv(sizes_ref[first + sector], STEP) * STEP for sector in range(sectors)
    ]
    return first, lambda sector: (
        sum(
            jnp.where(other < sector, lanes * height, 0)
            for other, height in enumerate(heights)
        ),
        sum(
            jnp.where(other == sector, height, 0) for other, height in enumerate(heights)
        ),
    )


def halve_kernel(
    sizes_ref, operators_ref, basis_ref, out_ref,
    blocks, own, turned, packed, block_sem, own_sem, out_sem,
):
    pairs, sectors, width = blocks.shape[0], blocks.shape[1], blocks.shape[3]
    count, rows = out_ref.shape[0], out_ref.shape[2]
    first, region = regions_of(sizes_ref, sectors, width // LANES)

    def fetch_own(sector):
        return pltpu.make_async_copy(
            basis_ref.at[sector], own.at[sector], own_sem.at[sector]
        )

    def fetch(pair, sector):
        return pltpu.make_async_copy(
            operators_ref.at[pair, sector],
            blocks.at[pair, sector],
            block_sem.at[pair * sectors + sector],
        )

    for pair in range(pairs):
        for sector in range(sectors):
            if pair == 0:
                fetch_own(sector).start()
            fetch(pair, sector).start()

    @pl.loop(0, pairs * sectors)
    def _(index):
        pair, sector = index // sectors, index % sectors
        start, height = region(sector)

        @pl.when(pair == 0)
        def _():
            fetch_own(sector).wait()
            for tile in range(width // TILE):
                span = slice(tile * TILE, (tile + 1) * TILE)
                place = tile * TILE + lax.broadcasted_iota(jnp.int32, (TILE, width), 0)
                strip = own[sector, :, span].T
                turned[sector, span, :] = jnp.where(
                    place < sizes_ref[first + sector], strip, jnp.zeros_like(strip)
                )

        fetch(pair, sector).wait()
        for tile in range(width // TILE):
            half = times_transposed(
                turned[sector], blocks[pair, sector, tile * TILE : (tile + 1) * TILE, :]
            ).astype(packed.dtype)
            for side in range(TILE // LANES):
                lane = tile * (TILE // LANES) + side
                packed[pair, pl.ds(pl.multiple_of(start + lane * height, STEP), width), :] = (
                    half[:, side * LANES : (side + 1) * LANES]
                )

        @pl.when(sector == sectors - 1)
        def _():
            @pl.loop(0, count)
            def _(part):
                pltpu.make_async_copy(
                    packed.at[pair, pl.ds(pl.multiple_of(part * rows, SUBLANES), rows)],
                    out_ref.at[part, pair],
                    out_sem,
                ).start()

    pltpu.make_async_copy(out_ref, out_ref, out_sem).wait()


def halve(sizes, operators, basis, count, rows):
    pairs, sectors, height, width = operators.shape
    dtype = operators.dtype
    return pl.pallas_call(
        halve_kernel,
        out_shape=jax.ShapeDtypeStruct((count, pairs, rows, LANES), dtype),
        in_specs=[SMEM, HBM, HBM],
        out_specs=HBM,
        scratch_shapes=[
            pltpu.VMEM(operators.shape, dtype),
            pltpu.VMEM(basis.shape, dtype),
            pltpu.VMEM((sectors, width, height), dtype),
            pltpu.VMEM((pairs, count * rows + width, LANES), dtype),
            pltpu.SemaphoreType.DMA((pairs * sectors,)),
            pltpu.SemaphoreType.DMA((sectors,)),
            pltpu.SemaphoreType.DMA,
        ],
        cost_estimate=pl.CostEstimate(
            flops=2 * operators.size * width,
            bytes_accessed=4 * operators.size,
            transcendentals=0,
        ),
        name="halve",
    )(sizes, operators, basis)


def finish_kernel(
    sizes_ref, offset_ref, strips_ref, turned_ref, out_ref,
    packed, target, half, result, in_sem, target_sem, out_sem,
):
    pairs, sectors, width = result.shape[0], result.shape[1], result.shape[3]
    count, rows = strips_ref.shape[0], strips_ref.shape[2]
    _, region = regions_of(sizes_ref, sectors, width // LANES)

    def fetch(pair, sector):
        slot = pair * sectors + sector
        return pltpu.make_async_copy(
            turned_ref.at[sector + 1 + offset_ref[pair]],
            target.at[slot],
            target_sem.at[slot],
        )

    for pair in range(pairs):

        @pl.loop(0, count)
        def _(part):
            pltpu.make_async_copy(
                strips_ref.at[part, pair],
                packed.at[pair, pl.ds(pl.multiple_of(part * rows, SUBLANES), rows)],
                in_sem.at[pair],
            ).start()

        for sector in range(sectors):
            fetch(pair, sector).start()

    @pl.loop(0, pairs * sectors)
    def _(index):
        pair, sector = index // sectors, index % sectors
        start, height = region(sector)

        @pl.when(sector == 0)
        def _():
            whole = packed.at[pair, pl.ds(0, count * rows)]
            pltpu.make_async_copy(whole, whole, in_sem.at[pair]).wait()

        for lane in range(width // LANES):
            half[:, lane * LANES : (lane + 1) * LANES] = packed[
                pair, pl.ds(pl.multiple_of(start + lane * height, STEP), width), :
            ]

        @pl.loop(height // STEP, width // STEP)
        def _(step):
            row = pl.multiple_of(step * STEP, STEP)
            half[pl.ds(row, STEP), :] = jnp.zeros((STEP, width), half.dtype)

        fetch(pair, sector).wait()
        for tile in range(width // TILE):
            span = slice(tile * TILE, (tile + 1) * TILE)
            result[pair, sector, :, span] = times_transposed(
                target[index], half[span, :]
            ).astype(result.dtype)
            pltpu.make_async_copy(
                result.at[pair, sector, :, span], out_ref.at[pair, sector, :, span], out_sem
            ).start()

    pltpu.make_async_copy(out_ref, out_ref, out_sem).wait()


def finish(sizes, offsets, strips, turned, shape):
    pairs, sectors, height, width = shape
    count, _, rows, _ = strips.shape
    dtype = strips.dtype
    size = pairs * sectors * height * width
    return pl.pallas_call(
        finish_kernel,
        out_shape=jax.ShapeDtypeStruct(shape, dtype),
        in_specs=[SMEM, SMEM, HBM, HBM],
        out_specs=HBM,
        scratch_shapes=[
            pltpu.VMEM((pairs, count * rows + width, LANES), dtype),
            pltpu.VMEM((pairs * sectors, height, width), dtype),
            pltpu.VMEM((width, height), dtype),
            pltpu.VMEM(shape, dtype),
            pltpu.SemaphoreType.DMA((pairs,)),
            pltpu.SemaphoreType.DMA((pairs * sectors,)),
            pltpu.SemaphoreType.DMA,
        ],
        cost_estimate=pl.CostEstimate(
            flops=2 * size * width, bytes_accessed=6 * size, transcendentals=0
        ),
        compiler_params=pltpu.CompilerParams(vmem_limit_bytes=24 << 20),
        name="finish",
    )(sizes, offsets, strips, turned)


def reorder_kernel(dest_ref, in_ref, out_ref, out_sem):
    @pl.loop(0, in_ref.shape[0])
    def _(pair):
        pltpu.make_async_copy(
            in_ref.at[pair], out_ref.at[dest_ref[pair]], out_sem
        ).start()

    pltpu.make_async_copy(out_ref, out_ref, out_sem).wait()


def reorder(blocks, dest):
    return pl.pallas_call(
        reorder_kernel,
        out_shape=jax.ShapeDtypeStruct(blocks.shape, blocks.dtype),
        in_specs=[SMEM, HBM],
        out_specs=HBM,
        scratch_shapes=[pltpu.SemaphoreType.DMA],
        cost_estimate=pl.CostEstimate(
            flops=0, bytes_accessed=4 * blocks.size, transcendentals=0
        ),
        compiler_params=pltpu.CompilerParams(vmem_limit_bytes=8 << 20),
        name="reorder",
    )(dest, blocks)


def turned_basis(basis, sector_sizes):
    sectors, width = basis.shape[0], basis.shape[2]
    sec_count, sec_pos = lax.axis_size("sec"), lax.axis_index("sec")
    total = sectors * sec_count
    forward = [(i, (i + 1) % sec_count) for i in range(sec_count)]
    backward = [(j, i) for i, j in forward]
    low = lax.ppermute(basis[-1:], "sec", forward)
    high = lax.ppermute(basis[:1], "sec", backward)
    near = jnp.concatenate([low, basis, high], axis=0)
    near_ids = (sec_pos * sectors - 1 + jnp.arange(sectors + 2, dtype=jnp.int32)) % total
    sizes = jnp.sum(
        jnp.where(
            near_ids[:, None] == jnp.arange(total, dtype=jnp.int32)[None, :],
            sector_sizes[None, :],
            0,
        ),
        axis=1,
    )
    kept = jnp.arange(width, dtype=jnp.int32)[None, :] < sizes[:, None]
    return jnp.swapaxes(jnp.where(kept[:, None, :], near, jnp.zeros_like(near)), 1, 2)


def pipeline(rows, operators, basis, shift, dest, sector_sizes):
    pairs = operators.shape[0]
    count = lax.axis_size("ops")
    strips = halve(sector_sizes, operators, basis, count, rows)
    spread = lax.all_to_all(strips, "ops", 0, 0, tiled=True)
    turned = turned_basis(basis, sector_sizes)
    mine = lax.axis_index("ops") * pairs + jnp.arange(pairs, dtype=jnp.int32)
    offsets = jnp.sum(jnp.where(mine[:, None] == dest[None, :], shift[None, :], 0), axis=1)
    spread, turned, offsets = lax.optimization_barrier((spread, turned, offsets))
    ordered = reorder(spread.reshape((count * pairs,) + spread.shape[2:]), dest)
    back = lax.all_to_all(ordered.reshape(spread.shape), "ops", 0, 0, tiled=True)
    return finish(sector_sizes, offsets, back, turned, operators.shape)


def body(operators, basis, shift, dest, sector_sizes):
    sectors, width = operators.shape[1], operators.shape[3]
    lanes, part = width // LANES, lax.axis_size("ops") * SUBLANES
    most = lanes * sectors * width // part
    least = most - CHOICES + 1
    heights = (sector_sizes + STEP - 1) // STEP * STEP
    longest = jnp.max(jnp.sum(heights.reshape(-1, sectors), axis=1)) * lanes
    choice = jnp.clip((longest + part - 1) // part - least, 0, CHOICES - 1)
    return lax.switch(
        choice,
        [
            functools.partial(pipeline, SUBLANES * tiles)
            for tiles in range(least, most + 1)
        ],
        operators, basis, shift, dest, sector_sizes,
    )


def solution(mesh):
    return jax.shard_map(
        body,
        mesh=mesh,
        in_specs=(P("ops", "sec", None, None), P("sec", None, None), P(), P(), P()),
        out_specs=P("ops", "sec", None, None),
        check_vma=False,
    )
```

profile of v0, /device:TPU:1, one launch (start us, length us, event | category | flops | bytes accessed | tf_op | source)
XLA Modules:
  0.0 252.5 jit_solution(5716407858101740755)
XLA Ops:
  0.0 0.7 fusion.12
  0.7 0.1 reshape.183
  0.8 0.1 reduce_sum.81
  0.9 0.6 reduce_max.9
  2.2 250.2 %conditional.1 = (bf16[2,2,768,768]{3,2,1,0:T(8,128)(2,1)}) conditional(s32[]{:T(128)} %clamp.3, (s32[8]{0:T(128)}, bf16[2,2,768,768]{3,2,1,0:T(8,128)(2,1)}, bf16[2,768,768]{2,1,0:T(8,128)(2,1)}, s32[128]{0:T(128)}, s32[128]{0:T(128)}) %tuple.21, (s32[8]{0:T(128)}, bf16[2,2,768,768]{3,2,1,0:T(8,128)(2,1)}, ...), branch_computations={%region_2.5_spmd, %region_5.8_spmd, %region_8.11_spmd, %region_11.... | conditional | flops 7254839296 | bytes 117976712 | solution.py:292
  2.4 10.0 %halve.6 = bf16[64,2,136,128]{3,2,1,0:T(8,128)(2,1)} custom-call(s32[8]{0:T(128)} %get-tuple-element.66.sizes_ref, bf16[2,2,768,768]{3,2,1,0:T(8,128)(2,1)} %get-tuple-element.101.operators_ref, bf16[2,768,768]{2,1,0:T(8,128)(2,1)} %get-tuple-element.167.basis_ref), custom_call_target="tpu_custom_call" | custom-call | flops 3623878656 | bytes 9437184 | tf_op jit(solution)/shard_map/cond/branch_2_fun/halve/pallas_call | solution.py:111
  12.4 0.0 copy-start.2
  12.4 13.3 %all-to-all-start.4 = ((bf16[64,2,136,128]{3,2,1,0:T(8,128)(2,1)}), bf16[64,2,136,128]{3,2,1,0:T(8,128)(2,1)}, u32[]{:S(2)}, u32[]{:S(2)}) async-start(bf16[64,2,136,128]{3,2,1,0:T(8,128)(2,1)} %halve.6), calls=%async_computation.4 | async-start | bytes 8912896 | tf_op jit(solution)/shard_map/cond/branch_2_fun/all_to_all | solution.py:274
  25.7 0.0 copy-done.2
  25.8 0.0 copy-start.18
  25.8 0.0 copy-start.10
  25.8 0.0 copy-start.14
  25.8 2.4 copy.48
  28.2 3.3 %fusion.15 = (bf16[1,768,768]{1,2,0:T(8,128)(2,1)}, bf16[1,768,768]{1,2,0:T(8,128)(2,1)}) fusion(bf16[2,768,768]{1,2,0:T(8,128)(2,1)} %copy.48), kind=kLoop, calls=%fused_computation.55 | loop fusion | bytes 4718592 | tf_op jit(solution)/shard_map/cond/branch_2_fun/slice | solution.py:254
  31.6 1.3 collective-permute-start.4
  32.8 1.4 collective-permute-start.5
  34.3 0.0 copy-done.18
  34.3 0.2 select_reduce_fusion.2
  34.5 0.0 copy-done.10
  34.5 0.0 copy-done.14
  34.5 0.2 fusion.7.offset_ref
  34.7 0.1 iota_compare_fusion.4
  34.8 25.4 %collective-permute-done.4 = bf16[1,768,768]{1,2,0:T(8,128)(2,1)S(1)} collective-permute-done((bf16[1,768,768]{1,2,0:T(8,128)(2,1)}, bf16[1,768,768]{1,2,0:T(8,128)(2,1)S(1)}, u32[]{:S(2)}, u32[]{:S(2)}) %collective-permute-start.4) | collective-permute-done | bytes 1179680 | tf_op jit(solution)/shard_map/cond/branch_2_fun/ppermute | solution.py:254
  60.2 0.0 collective-permute-done.5
  60.2 0.0 copy-done.6
  60.2 3.9 %fusion.6.turned_ref = bf16[4,768,768]{2,1,0:T(8,128)(2,1)} fusion(bf16[1,768,768]{1,2,0:T(8,128)(2,1)} %collective-permute-done.5, bf16[2,768,768]{1,2,0:T(8,128)(2,1)S(1)} %copy-done.6, bf16[1,768,768]{1,2,0:T(8,128)(2,1)S(1)} %collective-permute-done.4, pred[4,768]{1,0:T(4,128)(4,1)S(1)} %iota_compare_fusion.4), kind=kLoop, calls=%fused_computation.25 | loop fusion | flops 7077888 | bytes 9440256 | tf_op jit(solution)/shard_map/cond/branch_2_fun/transpose | solution.py:267
  64.2 63.1 %all-to-all-done.4 = bf16[64,2,136,128]{3,2,1,0:T(8,128)(2,1)} async-done(((bf16[64,2,136,128]{3,2,1,0:T(8,128)(2,1)}), bf16[64,2,136,128]{3,2,1,0:T(8,128)(2,1)}, u32[]{:S(2)}, u32[]{:S(2)}) %all-to-all-start.4) | async-done | bytes 4456480 | tf_op jit(solution)/shard_map/cond/branch_2_fun/all_to_all | solution.py:274
  127.2 3.1 %reorder.6 = bf16[128,136,128]{2,1,0:T(8,128)(2,1)S(1)} custom-call(s32[128]{0:T(128)S(1)} %copy-done.10, bf16[128,136,128]{2,1,0:T(8,128)(2,1)} %bitcast.7.in_ref), custom_call_target="tpu_custom_call" | custom-call | bytes 8912896 | tf_op jit(solution)/shard_map/cond/branch_2_fun/reorder/pallas_call | solution.py:234
  130.3 0.0 slice-start.5
  130.3 107.6 %all_to_all.34.strips_ref = bf16[64,2,136,128]{3,2,1,0:T(8,128)(2,1)S(1)} all-to-all(bf16[64,2,136,128]{3,2,1,0:T(8,128)(2,1)S(1)} %bitcast.23), channel_id=1, replica_groups=mesh['ops'=64,'sec'=4] {'ops'}, dimensions={0} | all-to-all | bytes 8912896 | tf_op jit(solution)/shard_map/cond/branch_2_fun/all_to_all | solution.py:280
  237.9 0.0 slice-done.5
  237.9 14.5 %finish.6 = bf16[2,2,768,768]{3,2,1,0:T(8,128)(2,1)} custom-call(s32[8]{0:T(128)S(1)} %copy-done.18, s32[2]{0:T(128)S(1)} %fusion.7.offset_ref, bf16[64,2,136,128]{3,2,1,0:T(8,128)(2,1)S(1)} %all_to_all.34.strips_ref, bf16[4,768,768]{2,1,0:T(8,128)(2,1)S(1)} %bitcast.22), custom_call_target="tpu_custom_call" | custom-call | flops 3623878656 | bytes 14155776 | tf_op jit(solution)/shard_map/cond/branch_2_fun/finish/pallas_call | solution.py:201
  (6 shorter events, 0.0 us)
Async XLA Ops:
  12.4 13.3 %copy-start.2 = (bf16[2,768,768]{2,1,0:T(8,128)(2,1)S(1)}, bf16[2,768,768]{2,1,0:T(8,128)(2,1)}, u32[]{:S(2)}) copy-start(bf16[2,768,768]{2,1,0:T(8,128)(2,1)} %get-tuple-element.167.basis_ref) | copy-start | bytes 7077892 | tf_op jit(solution)/shard_map/cond
  12.4 114.8 %all-to-all-start.4 = ((bf16[64,2,136,128]{3,2,1,0:T(8,128)(2,1)}), bf16[64,2,136,128]{3,2,1,0:T(8,128)(2,1)}, u32[]{:S(2)}, u32[]{:S(2)}) async-start(bf16[64,2,136,128]{3,2,1,0:T(8,128)(2,1)} %halve.6), calls=%async_computation.4 | async-start | bytes 8912896 | tf_op jit(solution)/shard_map/cond/branch_2_fun/all_to_all | solution.py:274
  25.8 8.6 %copy-start.18 = (s32[8]{0:T(128)S(1)}, s32[8]{0:T(128)}, u32[]{:S(2)}) copy-start(s32[8]{0:T(128)} %get-tuple-element.66.sizes_ref) | copy-start | bytes 100 | tf_op jit(solution)/shard_map/cond
  25.8 8.7 %copy-start.10 = (s32[128]{0:T(128)S(1)}, s32[128]{0:T(128)}, u32[]{:S(2)}) copy-start(s32[128]{0:T(128)} %get-tuple-element.109.dest_ref) | copy-start | bytes 1540 | tf_op jit(solution)/shard_map/cond
  25.8 8.7 %copy-start.14 = (s32[128]{0:T(128)S(1)}, s32[128]{0:T(128)}, u32[]{:S(2)}) copy-start(s32[128]{0:T(128)} %get-tuple-element.113) | copy-start | bytes 1540 | tf_op jit(solution)/shard_map/cond
  28.2 32.0 %copy-start.6 = (bf16[2,768,768]{1,2,0:T(8,128)(2,1)S(1)}, bf16[2,768,768]{1,2,0:T(8,128)(2,1)}, u32[]{:S(2)}) copy-start(bf16[2,768,768]{1,2,0:T(8,128)(2,1)} %copy.48) | copy-start | bytes 7077892 | tf_op jit(solution)/shard_map/cond
  31.6 28.7 %collective-permute-start.4 = (bf16[1,768,768]{1,2,0:T(8,128)(2,1)}, bf16[1,768,768]{1,2,0:T(8,128)(2,1)S(1)}, u32[]{:S(2)}, u32[]{:S(2)}) collective-permute-start(bf16[1,768,768]{1,2,0:T(8,128)(2,1)} %get-tuple-element.179), channel_id=1, source_target_pairs={{0,1},{1,2},{2,3},{3,0},{4,5},{5,6},{6,7},{7,4},{8,9},{9,10},{10,1... | collective-permute-start | bytes 3538952 | tf_op jit(solution)/shard_map/cond/branch_2_fun/ppermute | solution.py:254
  32.8 27.4 %collective-permute-start.5 = (bf16[1,768,768]{1,2,0:T(8,128)(2,1)}, bf16[1,768,768]{1,2,0:T(8,128)(2,1)}, u32[]{:S(2)}, u32[]{:S(2)}) collective-permute-start(bf16[1,768,768]{1,2,0:T(8,128)(2,1)} %get-tuple-element.180), channel_id=1, source_target_pairs={{1,0},{2,1},{3,2},{0,3},{5,4},{6,5},{7,6},{4,7},{9,8},{10,9},{11,1... | collective-permute-start | bytes 3538952 | tf_op jit(solution)/shard_map/cond/branch_2_fun/ppermute | solution.py:255
  127.2 110.7 %slice-start.4 = ((s8[4718592]{0:T(1024)(128)(4,1)}), s8[4194304]{0:T(1024)(128)(4,1)S(1)}, s32[]{:S(2)}) async-start(s8[4718592]{0:T(1024)(128)(4,1)} %bitcast.21), calls=%async_computation.12 | async-start | bytes 8388608 | tf_op jit(solution)/shard_map/cond
  130.3 107.6 %slice-start.5 = ((s8[4718592]{0:T(1024)(128)(4,1)}), s8[524288]{0:T(1024)(128)(4,1)S(1)}, s32[]{:S(2)}) async-start(s8[4718592]{0:T(1024)(128)(4,1)} %bitcast.21), calls=%async_computation.13 | async-start | bytes 1048576 | tf_op jit(solution)/shard_map/cond
where the time goes:
time: 253 us
  blocking collectives  108 us (43%)
  waiting for transfers between devices  88.5 us (35%)
  Pallas kernels  27.6 us (11%)
  starting transfers between devices  16 us (6%)
  local copies, waits for them, and re-layouts  5.88 us (2%)
  other arithmetic  5.81 us (2%)
    all_to_all x1, blocking collectives, pipeline(): lax.all_to_all(ordered.reshape(spread.shape), 'ops', 0, 0, tiled=True)  108 us
    all_to_all x1, waiting for transfers between devices, pipeline(): spread = lax.all_to_all(strips, 'ops', 0, 0, tiled=True)  63.1 us
    ppermute x1, waiting for transfers between devices, turned_basis(): low = lax.ppermute(basis[-1:], 'sec', forward)  25.4 us
    pallas_call x1, Pallas kernels, finish(): pl.pallas_call(finish_kernel, out_shape=jax.ShapeDtypeStruct(shape, dtype...  14.5 us
    all_to_all x1, starting transfers between devices, pipeline(): spread = lax.all_to_all(strips, 'ops', 0, 0, tiled=True)  13.3 us
    pallas_call x1, Pallas kernels, halve(): pl.pallas_call(halve_kernel, out_shape=jax.ShapeDtypeStruct((count, pairs...  10 us
  transfers between devices with their start and end apart: 3, of which 2 were waited for; matrix products, arithmetic and copies ran while one was open for 4% of the time, Pallas kernels for 0%

commit v1 on v0

--- a/solution.py
+++ b/solution.py
@@ -40,12 +40,13 @@
 
 
 def halve_kernel(
-    sizes_ref, operators_ref, basis_ref, out_ref,
-    blocks, own, turned, packed, block_sem, own_sem, out_sem,
+    sizes_hbm, operators_ref, basis_ref, out_ref,
+    sizes_ref, blocks, own, turned, packed, size_sem, block_sem, own_sem, out_sem,
 ):
     pairs, sectors, width = blocks.shape[0], blocks.shape[1], blocks.shape[3]
     count, rows = out_ref.shape[0], out_ref.shape[2]
-    first, region = regions_of(sizes_ref, sectors, width // LANES)
+    sizes_copy = pltpu.make_async_copy(sizes_hbm, sizes_ref, size_sem)
+    sizes_copy.start()
 
     def fetch_own(sector):
         return pltpu.make_async_copy(
@@ -64,6 +65,9 @@
             if pair == 0:
                 fetch_own(sector).start()
             fetch(pair, sector).start()
+
+    sizes_copy.wait()
+    first, region = regions_of(sizes_ref, sectors, width // LANES)
 
     @pl.loop(0, pairs * sectors)
     def _(index):
@@ -111,13 +115,15 @@
     return pl.pallas_call(
         halve_kernel,
         out_shape=jax.ShapeDtypeStruct((count, pairs, rows, LANES), dtype),
-        in_specs=[SMEM, HBM, HBM],
+        in_specs=[HBM, HBM, HBM],
         out_specs=HBM,
         scratch_shapes=[
+            pltpu.SMEM(sizes.shape, sizes.dtype),
             pltpu.VMEM(operators.shape, dtype),
             pltpu.VMEM(basis.shape, dtype),
             pltpu.VMEM((sectors, width, height), dtype),
             pltpu.VMEM((pairs, count * rows + width, LANES), dtype),
+            pltpu.SemaphoreType.DMA,
             pltpu.SemaphoreType.DMA((pairs * sectors,)),
             pltpu.SemaphoreType.DMA((sectors,)),
             pltpu.SemaphoreType.DMA,
@@ -132,12 +138,16 @@
 
 
 def finish_kernel(
-    sizes_ref, offset_ref, strips_ref, turned_ref, out_ref,
-    packed, target, half, result, in_sem, target_sem, out_sem,
+    sizes_hbm, offset_hbm, strips_ref, turned_ref, out_ref,
+    sizes_ref, offset_ref, packed, target, half, result,
+    size_sem, offset_sem, in_sem, target_sem, out_sem,
 ):
     pairs, sectors, width = result.shape[0], result.shape[1], result.shape[3]
     count, rows = strips_ref.shape[0], strips_ref.shape[2]
-    _, region = regions_of(sizes_ref, sectors, width // LANES)
+    sizes_copy = pltpu.make_async_copy(sizes_hbm, sizes_ref, size_sem)
+    sizes_copy.start()
+    offset_copy = pltpu.make_async_copy(offset_hbm, offset_ref, offset_sem)
+    offset_copy.start()
 
     def fetch(pair, sector):
         slot = pair * sectors + sector
@@ -157,8 +167,13 @@
                 in_sem.at[pair],
             ).start()
 
+        if pair == 0:
+            offset_copy.wait()
         for sector in range(sectors):
             fetch(pair, sector).start()
+
+    sizes_copy.wait()
+    _, region = regions_of(sizes_ref, sectors, width // LANES)
 
     @pl.loop(0, pairs * sectors)
     def _(index):
@@ -201,13 +216,17 @@
     return pl.pallas_call(
         finish_kernel,
         out_shape=jax.ShapeDtypeStruct(shape, dtype),
-        in_specs=[SMEM, SMEM, HBM, HBM],
+        in_specs=[HBM, HBM, HBM, HBM],
         out_specs=HBM,
         scratch_shapes=[
+            pltpu.SMEM(sizes.shape, sizes.dtype),
+            pltpu.SMEM(offsets.shape, offsets.dtype),
             pltpu.VMEM((pairs, count * rows + width, LANES), dtype),
             pltpu.VMEM((pairs * sectors, height, width), dtype),
             pltpu.VMEM((width, height), dtype),
             pltpu.VMEM(shape, dtype),
+            pltpu.SemaphoreType.DMA,
+            pltpu.SemaphoreType.DMA,
             pltpu.SemaphoreType.DMA((pairs,)),
             pltpu.SemaphoreType.DMA((pairs * sectors,)),
             pltpu.SemaphoreType.DMA,
@@ -215,13 +234,12 @@
         cost_estimate=pl.CostEstimate(
             flops=2 * size * width, bytes_accessed=6 * size, transcendentals=0
         ),
-        compiler_params=pltpu.CompilerParams(vmem_limit_bytes=24 << 20),
         name="finish",
     )(sizes, offsets, strips, turned)
 
 
 def reorder_kernel(dest_ref, in_ref, out_ref, out_sem):
-    @pl.loop(0, in_ref.shape[0])
+    @pl.loop(0, in_ref.shape[0], unroll=8)
     def _(pair):
         pltpu.make_async_copy(
             in_ref.at[pair], out_ref.at[dest_ref[pair]], out_sem

time: 253 us -> 246 us (0.972)
  Pallas kernels: 27.6 us -> 20.8 us
    pallas_call x1, Pallas kernels: 14.5 us -> 8.76 us  [finish(): pl.pallas_call(finish_kernel, out_shape=jax.ShapeDtypeStruct(shape, dtype...]
where the time goes in v1:
time: 246 us
  blocking collectives  108 us (44%)
  waiting for transfers between devices  88 us (36%)
  Pallas kernels  20.8 us (8%)
  starting transfers between devices  16 us (7%)
  other arithmetic  6.32 us (3%)
  local copies, waits for them, and re-layouts  5.92 us (2%)
    all_to_all x1, blocking collectives, pipeline(): lax.all_to_all(ordered.reshape(spread.shape), 'ops', 0, 0, tiled=True)  108 us
    all_to_all x1, waiting for transfers between devices, pipeline(): spread = lax.all_to_all(strips, 'ops', 0, 0, tiled=True)  63 us
    ppermute x1, waiting for transfers between devices, turned_basis(): low = lax.ppermute(basis[-1:], 'sec', forward)  24.9 us
    all_to_all x1, starting transfers between devices, pipeline(): spread = lax.all_to_all(strips, 'ops', 0, 0, tiled=True)  13.3 us
    pallas_call x1, Pallas kernels, halve(): pl.pallas_call(halve_kernel, out_shape=jax.ShapeDtypeStruct((count, pairs...  9.29 us
    pallas_call x1, Pallas kernels, finish(): pl.pallas_call(finish_kernel, out_shape=jax.ShapeDtypeStruct(shape, dtype...  8.76 us
  transfers between devices with their start and end apart: 3, of which 2 were waited for; matrix products, arithmetic and copies ran while one was open for 4% of the time, Pallas kernels for 0%

profile of v1, /device:TPU:1, one launch (start us, length us, event | category | flops | bytes accessed | tf_op | source)
XLA Modules:
  0.0 245.7 jit_solution(7946160586549258648)
XLA Ops:
  0.0 0.7 fusion.12
  0.7 0.1 reshape.183
  0.8 0.1 reduce_sum.81
  0.9 0.6 reduce_max.9
  2.2 243.4 %conditional.1 = (bf16[2,2,768,768]{3,2,1,0:T(8,128)(2,1)}) conditional(s32[]{:T(128)} %clamp.3, (s32[8]{0:T(128)}, bf16[2,2,768,768]{3,2,1,0:T(8,128)(2,1)}, bf16[2,768,768]{2,1,0:T(8,128)(2,1)}, s32[128]{0:T(128)}, s32[128]{0:T(128)}) %tuple.21, (s32[8]{0:T(128)}, bf16[2,2,768,768]{3,2,1,0:T(8,128)(2,1)}, ...), branch_computations={%region_2.5_spmd, %region_5.8_spmd, %region_8.11_spmd, %region_11.... | conditional | flops 7254839296 | bytes 103820888 | solution.py:310
  2.4 9.3 %halve.6 = bf16[64,2,136,128]{3,2,1,0:T(8,128)(2,1)} custom-call(s32[8]{0:T(128)} %get-tuple-element.66.sizes_hbm, bf16[2,2,768,768]{3,2,1,0:T(8,128)(2,1)} %get-tuple-element.101.operators_ref, bf16[2,768,768]{2,1,0:T(8,128)(2,1)} %get-tuple-element.167.basis_ref), custom_call_target="tpu_custom_call" | custom-call | flops 3623878656 | bytes 9437184 | tf_op jit(solution)/shard_map/cond/branch_2_fun/halve/pallas_call | solution.py:115
  11.7 0.0 copy-start.2
  11.7 13.3 %all-to-all-start.4 = ((bf16[64,2,136,128]{3,2,1,0:T(8,128)(2,1)}), bf16[64,2,136,128]{3,2,1,0:T(8,128)(2,1)}, u32[]{:S(2)}, u32[]{:S(2)}) async-start(bf16[64,2,136,128]{3,2,1,0:T(8,128)(2,1)} %halve.6), calls=%async_computation.4 | async-start | bytes 8912896 | tf_op jit(solution)/shard_map/cond/branch_2_fun/all_to_all | solution.py:292
  25.0 0.0 copy-done.2
  25.0 0.0 copy-start.18
  25.0 0.0 copy-start.10
  25.0 0.0 copy-start.14
  25.0 2.5 %copy.48 = bf16[2,768,768]{1,2,0:T(8,128)(2,1)} copy(bf16[2,768,768]{2,1,0:T(8,128)(2,1)S(1)} %copy-done.2) | data formatting | bytes 4718592 | tf_op jit(solution)/shard_map
  27.5 0.0 copy-start.6
  27.5 3.3 %fusion.15 = (bf16[1,768,768]{1,2,0:T(8,128)(2,1)}, bf16[1,768,768]{1,2,0:T(8,128)(2,1)}) fusion(bf16[2,768,768]{1,2,0:T(8,128)(2,1)} %copy.48), kind=kLoop, calls=%fused_computation.55 | loop fusion | bytes 4718592 | tf_op jit(solution)/shard_map/cond/branch_2_fun/slice | solution.py:272
  30.8 1.3 collective-permute-start.4
  32.1 1.4 collective-permute-start.5
  33.6 0.0 copy-done.18
  33.6 0.2 select_reduce_fusion.2
  33.8 0.0 copy-done.10
  33.8 0.0 copy-done.14
  33.8 0.7 fusion.7.offset_hbm
  34.5 0.1 iota_compare_fusion.4
  34.6 24.9 %collective-permute-done.4 = bf16[1,768,768]{1,2,0:T(8,128)(2,1)S(1)} collective-permute-done((bf16[1,768,768]{1,2,0:T(8,128)(2,1)}, bf16[1,768,768]{1,2,0:T(8,128)(2,1)S(1)}, u32[]{:S(2)}, u32[]{:S(2)}) %collective-permute-start.4) | collective-permute-done | bytes 1179680 | tf_op jit(solution)/shard_map/cond/branch_2_fun/ppermute | solution.py:272
  59.5 0.0 collective-permute-done.5
  59.5 0.0 copy-done.6
  59.5 3.9 %fusion.6.turned_ref = bf16[4,768,768]{2,1,0:T(8,128)(2,1)} fusion(bf16[1,768,768]{1,2,0:T(8,128)(2,1)} %collective-permute-done.5, bf16[2,768,768]{1,2,0:T(8,128)(2,1)S(1)} %copy-done.6, bf16[1,768,768]{1,2,0:T(8,128)(2,1)S(1)} %collective-permute-done.4, pred[4,768]{1,0:T(4,128)(4,1)S(1)} %iota_compare_fusion.4), kind=kLoop, calls=%fused_computation.25 | loop fusion | flops 7077888 | bytes 9440256 | tf_op jit(solution)/shard_map/cond/branch_2_fun/transpose | solution.py:285
  63.5 63.0 %all-to-all-done.4 = bf16[64,2,136,128]{3,2,1,0:T(8,128)(2,1)} async-done(((bf16[64,2,136,128]{3,2,1,0:T(8,128)(2,1)}), bf16[64,2,136,128]{3,2,1,0:T(8,128)(2,1)}, u32[]{:S(2)}, u32[]{:S(2)}) %all-to-all-start.4) | async-done | bytes 4456480 | tf_op jit(solution)/shard_map/cond/branch_2_fun/all_to_all | solution.py:292
  126.5 2.8 %reorder.6 = bf16[128,136,128]{2,1,0:T(8,128)(2,1)S(1)} custom-call(s32[128]{0:T(128)S(1)} %copy-done.10, bf16[128,136,128]{2,1,0:T(8,128)(2,1)} %bitcast.7.in_ref), custom_call_target="tpu_custom_call" | custom-call | bytes 8912896 | tf_op jit(solution)/shard_map/cond/branch_2_fun/reorder/pallas_call | solution.py:252
  129.3 107.5 %all_to_all.34.strips_ref = bf16[64,2,136,128]{3,2,1,0:T(8,128)(2,1)} all-to-all(bf16[64,2,136,128]{3,2,1,0:T(8,128)(2,1)S(1)} %bitcast.17), channel_id=1, replica_groups=mesh['ops'=64,'sec'=4] {'ops'}, dimensions={0} | all-to-all | bytes 8912896 | tf_op jit(solution)/shard_map/cond/branch_2_fun/all_to_all | solution.py:298
  236.8 8.8 %finish.6 = bf16[2,2,768,768]{3,2,1,0:T(8,128)(2,1)} custom-call(s32[8]{0:T(128)S(1)} %copy-done.18, s32[2]{0:T(128)} %fusion.7.offset_hbm, bf16[64,2,136,128]{3,2,1,0:T(8,128)(2,1)} %all_to_all.34.strips_ref, bf16[4,768,768]{2,1,0:T(8,128)(2,1)} %fusion.6.turned_ref), custom_call_target="tpu_custom_call" | custom-call | flops 3623878656 | bytes 14155776 | tf_op jit(solution)/shard_map/cond/branch_2_fun/finish/pallas_call | solution.py:216
  (2 shorter events, 0.0 us)
Async XLA Ops:
  11.7 13.3 %copy-start.2 = (bf16[2,768,768]{2,1,0:T(8,128)(2,1)S(1)}, bf16[2,768,768]{2,1,0:T(8,128)(2,1)}, u32[]{:S(2)}) copy-start(bf16[2,768,768]{2,1,0:T(8,128)(2,1)} %get-tuple-element.167.basis_ref) | copy-start | bytes 7077892 | tf_op jit(solution)/shard_map/cond
  11.7 114.8 %all-to-all-start.4 = ((bf16[64,2,136,128]{3,2,1,0:T(8,128)(2,1)}), bf16[64,2,136,128]{3,2,1,0:T(8,128)(2,1)}, u32[]{:S(2)}, u32[]{:S(2)}) async-start(bf16[64,2,136,128]{3,2,1,0:T(8,128)(2,1)} %halve.6), calls=%async_computation.4 | async-start | bytes 8912896 | tf_op jit(solution)/shard_map/cond/branch_2_fun/all_to_all | solution.py:292
  25.0 8.6 %copy-start.18 = (s32[8]{0:T(128)S(1)}, s32[8]{0:T(128)}, u32[]{:S(2)}) copy-start(s32[8]{0:T(128)} %get-tuple-element.66.sizes_hbm) | copy-start | bytes 100 | tf_op jit(solution)/shard_map/cond
  25.0 8.8 %copy-start.10 = (s32[128]{0:T(128)S(1)}, s32[128]{0:T(128)}, u32[]{:S(2)}) copy-start(s32[128]{0:T(128)} %get-tuple-element.109.dest_ref) | copy-start | bytes 1540 | tf_op jit(solution)/shard_map/cond
  25.0 8.8 %copy-start.14 = (s32[128]{0:T(128)S(1)}, s32[128]{0:T(128)}, u32[]{:S(2)}) copy-start(s32[128]{0:T(128)} %get-tuple-element.113) | copy-start | bytes 1540 | tf_op jit(solution)/shard_map/cond
  27.5 32.0 %copy-start.6 = (bf16[2,768,768]{1,2,0:T(8,128)(2,1)S(1)}, bf16[2,768,768]{1,2,0:T(8,128)(2,1)}, u32[]{:S(2)}) copy-start(bf16[2,768,768]{1,2,0:T(8,128)(2,1)} %copy.48) | copy-start | bytes 7077892 | tf_op jit(solution)/shard_map/cond
  30.8 28.7 %collective-permute-start.4 = (bf16[1,768,768]{1,2,0:T(8,128)(2,1)}, bf16[1,768,768]{1,2,0:T(8,128)(2,1)S(1)}, u32[]{:S(2)}, u32[]{:S(2)}) collective-permute-start(bf16[1,768,768]{1,2,0:T(8,128)(2,1)} %get-tuple-element.179), channel_id=1, source_target_pairs={{0,1},{1,2},{2,3},{3,0},{4,5},{5,6},{6,7},{7,4},{8,9},{9,10},{10,1... | collective-permute-start | bytes 3538952 | tf_op jit(solution)/shard_map/cond/branch_2_fun/ppermute | solution.py:272
  32.1 27.4 %collective-permute-start.5 = (bf16[1,768,768]{1,2,0:T(8,128)(2,1)}, bf16[1,768,768]{1,2,0:T(8,128)(2,1)}, u32[]{:S(2)}, u32[]{:S(2)}) collective-permute-start(bf16[1,768,768]{1,2,0:T(8,128)(2,1)} %get-tuple-element.180), channel_id=1, source_target_pairs={{1,0},{2,1},{3,2},{0,3},{5,4},{6,5},{7,6},{4,7},{9,8},{10,9},{11,1... | collective-permute-start | bytes 3538952 | tf_op jit(solution)/shard_map/cond/branch_2_fun/ppermute | solution.py:273
